TPU v7x, 32 devices: a whole 2x2x4 slice. The times are simulated.
32 devices in a mesh: mem: 4 (over x, core), lat: 8 (over z, y).
Axes of the slice: x: 2, y: 2, z: 4, core: 2. Of those that a mesh axis runs over, the one named last changes fastest.
Arguments:
- control: bfloat16 [8, 10, 704, 1440], P('mem', None, 'lat'), may hold values from -6 to 6
- perturb: bfloat16 [8, 10, 704, 1440], P('mem', None, None, 'lat'), may hold values from -6 to 6
- lon_loc: bfloat16 [1440, 1440], P(None, 'mem'), may hold values from 0 to 1, as said below
- lat_loc: bfloat16 [704, 704], P('mem'), may hold values from 0 to 1, as said below
- static_scale: float32 [10, 704, 1440], P(None, 'mem', 'lat'), may hold values from 0.3 to 1
- static_field: float32 [10, 704, 1440], P(None, 'mem', 'lat'), may hold values from -6 to 6
- courant: float32 [2, 704, 1440], P(None, 'mem', 'lat'), may hold values from -0.48 to 0.48
Outputs:
- increment: float32 [10, 704, 1440], P(None, 'mem', 'lat')
- evolved: float32 [10, 704, 1440], P(None, 'mem', 'lat')
Inputs may be any that keep to these rules, and one draw needn't show every extreme that they name: `lon_loc`: Symmetric, with positive entries. `lat_loc`: Symmetric, with positive entries.
All inputs are finite; a program needn't handle non-finite values.
Results may differ from a plain program's by a relative error of at most 0.0027.
Values may be sent and summed in bfloat16 or wider, within the bound.
No kernel may reach another device: no remote copies, remote signals or barrier semaphores. Data moves between devices by JAX's collectives and lax.ppermute only.
A program may use at most 128 MiB of HBM per device.

v0:
```python
import math
import jax
import jax.numpy as jnp
from jax import lax
from jax.sharding import PartitionSpec as P

NLAT = 704
STEPS = 4


def padded_2(shard, sides, width, wrap):
    for axis, dim in sides:
        size, length = (lax.axis_size(axis), shard.shape[dim])
        up = [(i, (i + 1) % size) for i in range(size if wrap else size - 1)]
        down = [(j, i) for i, j in up]
        last = lax.slice_in_dim(shard, length - width, length, axis=dim)
        leading = lax.slice_in_dim(shard, 0, width, axis=dim)
        before = lax.ppermute(last, axis, up)
        after = lax.ppermute(leading, axis, down)
        shard = jnp.concatenate([before, shard, after], axis=dim)
    return shard


def upwind(padded, east_west, north_south):
    center = padded[:, 1:-1, 1:-1]
    western = padded[:, 1:-1, :-2]
    eastern = padded[:, 1:-1, 2:]
    southern = padded[:, :-2, 1:-1]
    northern = padded[:, 2:, 1:-1]
    zonal = jnp.maximum(east_west, 0.0) * (center - western) + jnp.minimum(east_west, 0.0) * (
        eastern - center
    )
    meridional = jnp.maximum(north_south, 0.0) * (center - southern) + jnp.minimum(
        north_south, 0.0
    ) * (northern - center)
    return center - zonal - meridional


def lon_rim(values, width):
    return padded_2(values, (("lat", 2),), width, True)


def lat_rim(values, width):
    return padded_2(values, (("mem", 1),), width, False)


def evolve(current, courant):
    fields = current.shape[0]
    stacked = jnp.concatenate([current, courant], axis=0)
    extended = lat_rim(lon_rim(stacked, STEPS), STEPS)
    result = extended[:fields]
    wind_ext = extended[fields:]
    for step_index in range(STEPS):
        margin = step_index + 1
        inner_wind = wind_ext[
            :, margin : wind_ext.shape[1] - margin, margin : wind_ext.shape[2] - margin
        ]
        result = upwind(result, inner_wind[0], inner_wind[1])
    return result


def per_device(control, perturb, lon_loc, lat_loc, static_scale, static_field, courant):
    along_lon = jnp.einsum(
        "mfal,lc->amfc",
        control,
        lax.all_gather(lon_loc, "mem", axis=1, tiled=True),
        preferred_element_type=jnp.float32,
    ).astype(jnp.bfloat16)
    banded = lax.all_to_all(along_lon, "lat", split_axis=3, concat_axis=0, tiled=True)
    mem_here = banded.shape[1]
    fields = banded.shape[2]
    lon_width = banded.shape[3]
    flat_band = banded.reshape(banded.shape[0], mem_here * fields * lon_width)
    pert_rows = jnp.transpose(perturb, (2, 0, 1, 3))
    lat_weights_all = lax.all_gather(lat_loc, "mem", axis=0, tiled=True)
    members = mem_here * lax.axis_size("mem")
    ens_scale = 1.0 / math.sqrt(members - 1)
    rows_own = NLAT // lax.axis_size("mem")
    localized = jnp.dot(lat_weights_all, flat_band, preferred_element_type=jnp.float32)
    localized = localized.reshape(NLAT, mem_here, fields, lon_width)
    ensemble_all = jnp.transpose(
        lax.psum(jnp.sum(localized * pert_rows.astype(jnp.float32), axis=1) * ens_scale, "mem"),
        (1, 0, 2),
    )
    offset = lax.axis_index("mem") * rows_own
    ensemble = lax.dynamic_slice_in_dim(ensemble_all, offset, rows_own, 1)
    increment = ensemble + static_scale * static_field
    evolved = evolve(increment, courant)
    return (increment, evolved)


def solution(mesh):
    placed = (
        P("mem", None, "lat", None),
        P("mem", None, None, "lat"),
        P(None, "mem"),
        P("mem", None),
        P(None, "mem", "lat"),
        P(None, "mem", "lat"),
        P(None, "mem", "lat"),
    )
    return jax.shard_map(
        per_device,
        mesh=mesh,
        in_specs=placed,
        out_specs=(P(None, "mem", "lat"), P(None, "mem", "lat")),
        check_vma=False,
    )
```

profile of v0, /device:TPU:1, one launch (start us, length us, event | category | flops | bytes accessed | tf_op | source)
XLA Modules:
  0.0 472.6 jit_solution(8537434043374464706)
XLA Ops:
  7.2 0.0 all-gather.2.cloned.1.call-start
  7.2 2.4 copy.32
  9.6 0.0 all-gather.2.cloned.1.call-update
  9.6 38.8 %all-gather.2.cloned.1.call-done = bf16[1440,1440]{0,1:T(8,128)(2,1)} async-done(((bf16[1440,360]{0,1:T(8,128)(2,1)}), bf16[1440,1440]{0,1:T(8,128)(2,1)}) %all-gather.2.cloned.1.call-update) | async-done | bytes 4147216 | tf_op jit(solution)/shard_map/all_gather | solution.py:66
  48.4 13.5 %convert_bitcast_fusion = bf16[88,2,10,1440]{3,0,2,1:T(8,128)(2,1)} fusion(bf16[2,10,88,1440]{3,2,1,0:T(8,128)(2,1)} %param.7, bf16[1440,1440]{0,1:T(8,128)(2,1)} %all-gather.2.cloned.1.call-done), kind=kOutput, calls=%fused_computation.4 | convolution fusion | flops 7301606400 | bytes 14284800 | tf_op jit(solution)/shard_map/mfal,lc->amfc/dot_general | solution.py:63
  61.8 16.8 %copy.34 = bf16[88,2,10,1440]{0,1,2,3:T(2,128)(2,1)} copy(bf16[88,2,10,1440]{3,0,2,1:T(8,128)(2,1)} %convert_bitcast_fusion) | data formatting | bytes 10137600 | tf_op jit(solution)/shard_map/convert_element_type | solution.py:68
  78.6 5.4 %all-to-all-start = ((bf16[88,2,10,1440]{0,1,2,3:T(2,128)(2,1)}), bf16[88,2,10,1440]{0,1,2,3:T(2,128)(2,1)}, u32[]{:S(2)}, u32[]{:S(2)}) async-start(bf16[88,2,10,1440]{0,1,2,3:T(2,128)(2,1)} %copy.34), calls=%async_computation | async-start | bytes 14745600 | tf_op jit(solution)/shard_map/all_to_all | solution.py:69
  84.0 0.0 all-reduce.2.cloned.1.call-start
  84.0 0.0 copy-done.7
  84.0 10.5 %all_gather.7 = bf16[704,704]{1,0:T(8,128)(2,1)S(1)} all-gather(bf16[176,704]{1,0:T(8,128)(2,1)S(1)} %copy-done.7), channel_id=1, replica_groups=mesh['mem'=4,'lat'=8] {'mem'}, dimensions={0}, use_global_device_ids=true | all-gather | bytes 1239040 | tf_op jit(solution)/shard_map/all_gather | solution.py:75
  94.5 150.4 %all-to-all-done = bf16[88,2,10,1440]{0,1,2,3:T(2,128)(2,1)} async-done(((bf16[88,2,10,1440]{0,1,2,3:T(2,128)(2,1)}), bf16[88,2,10,1440]{0,1,2,3:T(2,128)(2,1)}, u32[]{:S(2)}, u32[]{:S(2)}) %all-to-all-start) | async-done | bytes 5068832 | tf_op jit(solution)/shard_map/all_to_all | solution.py:69
  245.0 8.0 %copy.59 = bf16[88,2,10,8,180]{0,3,4,2,1:T(8,128)(2,1)} copy(bf16[88,2,10,8,180]{0,1,2,4,3:T(2,128)(2,1)} %bitcast.2) | data formatting | bytes 10137600 | tf_op jit(solution)/shard_map/all_to_all | solution.py:69
  253.0 12.2 %reshape.11 = bf16[704,3600]{0,1:T(8,128)(2,1)} reshape(bf16[8,88,2,10,180]{1,0,4,3,2:T(8,128)(2,1)} %bitcast.58) | data formatting | bytes 10137600 | tf_op jit(solution)/shard_map/reshape | solution.py:73
  265.2 9.6 %convolution_bitcast_fusion = f32[704,3600]{1,0:T(8,128)} fusion(bf16[704,3600]{0,1:T(8,128)(2,1)} %reshape.11, bf16[704,704]{1,0:T(8,128)(2,1)S(1)} %all_gather.7), kind=kOutput, calls=%fused_computation.3 | convolution fusion | flops 3568435200 | bytes 16197632 | tf_op jit(solution)/shard_map/dot_general | solution.py:79
  274.7 11.8 %copy.36 = f32[704,3600]{0,1:T(8,128)} copy(f32[704,3600]{1,0:T(8,128)} %convolution_bitcast_fusion) | data formatting | bytes 20275200 | tf_op jit(solution)/shard_map/dot_general | solution.py:79
  286.6 11.6 %reshape.12 = f32[704,2,10,180]{0,3,2,1:T(8,128)} reshape(f32[704,3600]{0,1:T(8,128)} %copy.36) | data formatting | bytes 20275200 | tf_op jit(solution)/shard_map/reshape | solution.py:80
  298.1 10.3 %fusion = f32[704,10,180]{0,2,1:T(8,128)} fusion(f32[704,2,10,180]{0,3,2,1:T(8,128)} %reshape.12, bf16[2,10,704,180]{2,0,3,1:T(2,128)(2,1)} %param.8), kind=kLoop, calls=%fused_computation.1 | loop fusion | flops 6336000 | bytes 20275200 | tf_op jit(solution)/shard_map/reduce_sum | solution.py:82
  308.4 5.5 %broadcast_multiply_fusion = f32[704,10,180]{0,2,1:T(8,128)} fusion(f32[704,10,180]{0,2,1:T(8,128)} %fusion), kind=kLoop, calls=%fused_computation.6 | loop fusion | flops 1267200 | bytes 10137600 | tf_op jit(solution)/shard_map/mul | solution.py:82
  313.9 0.0 all-reduce.2.cloned.1.call-update
  314.0 1.5 copy-done.1
  315.4 1.8 copy.38
  317.3 3.0 copy.39
  320.3 0.0 copy-done.2
  320.3 0.2 copy.40
  320.5 101.5 %all-reduce.2.cloned.1.call-done = f32[704,10,180]{0,2,1:T(8,128)} async-done(((f32[704,10,180]{0,2,1:T(8,128)}), f32[704,10,180]{0,2,1:T(8,128)}) %all-reduce.2.cloned.1.call-update) | async-done | bytes 5068816 | tf_op jit(solution)/shard_map/psum | solution.py:82
  422.0 3.5 bitcast_add_fusion
  425.6 1.2 collective-permute-start
  426.8 3.0 collective-permute-start.1
  429.8 1.6 collective-permute-done
  431.5 0.0 collective-permute-done.1
  431.6 0.3 pad_maximum_fusion
  431.8 1.4 fusion.34
  433.2 2.4 copy.45
  435.6 4.1 collective-permute-start.2
  439.7 1.1 copy.46
  440.8 2.1 collective-permute-start.3
  443.0 1.1 maximum_bitcast_fusion.7
  444.0 0.8 copy.49
  444.8 0.8 copy.50
  445.6 0.8 copy.51
  446.4 0.8 copy.52
  447.2 1.8 copy.53
  449.0 0.0 collective-permute-done.2
  449.0 1.2 copy.47
  450.2 0.0 collective-permute-done.3
  450.3 2.2 copy.48
  452.5 1.3 maximum_bitcast_fusion.3
  453.8 0.0 copy-done
  453.9 0.3 maximum_bitcast_fusion.5
  454.1 0.3 maximum_bitcast_fusion.1
  454.4 1.0 pad_maximum_fusion.1
  455.6 2.1 fusion.4
  457.7 2.0 fusion.28
  459.7 0.0 copy-start.3
  459.7 0.0 copy-start.4
  459.7 0.0 copy-start.5
  459.7 0.0 copy-start.6
  459.8 2.0 fusion.20
  461.8 0.0 copy-done.3
  461.8 0.0 copy-done.4
  461.8 0.0 copy-done.5
  461.8 0.0 copy-done.6
  461.8 2.1 fusion.12
  463.9 1.8 copy.54
  (12 shorter events, 0.2 us)
Async XLA Ops:
  7.2 41.2 %all-gather.2.cloned.1.call-start = ((), (), s32[]{:S(2)}) async-start(), calls=%async_computation.1 | async-start | bytes 5529600 | tf_op jit(solution)/shard_map/all_gather | solution.py:66
  78.6 5.4 %copy-start.7 = (bf16[176,704]{1,0:T(8,128)(2,1)S(1)}, bf16[176,704]{1,0:T(8,128)(2,1)}, u32[]{:S(2)}) copy-start(bf16[176,704]{1,0:T(8,128)(2,1)} %param.10) | copy-start | bytes 743428
  78.6 166.4 %all-to-all-start = ((bf16[88,2,10,1440]{0,1,2,3:T(2,128)(2,1)}), bf16[88,2,10,1440]{0,1,2,3:T(2,128)(2,1)}, u32[]{:S(2)}, u32[]{:S(2)}) async-start(bf16[88,2,10,1440]{0,1,2,3:T(2,128)(2,1)} %copy.34), calls=%async_computation | async-start | bytes 14745600 | tf_op jit(solution)/shard_map/all_to_all | solution.py:69
  84.0 338.0 %all-reduce.2.cloned.1.call-start = ((), (), s32[]{:S(2)}) async-start(), calls=%async_computation.2 | async-start | bytes 11304960 | tf_op jit(solution)/shard_map/psum | solution.py:82
  313.9 1.5 copy-start.1
  317.3 3.0 copy-start.2
  425.6 5.9 %collective-permute-start = (f32[12,176,4]{1,0,2:T(8,128)S(1)}, f32[12,176,4]{1,0,2:T(8,128)S(1)}, u32[]{:S(2)}, u32[]{:S(2)}) collective-permute-start(f32[12,176,4]{1,0,2:T(8,128)S(1)} %copy.41), channel_id=1, source_target_pairs={{0,1},{1,2},{2,3},{3,4},{4,5},{5,6},{6,7},{7,0},{8,9},{9,10},{10,1... | collective-permute-start | bytes 101384 | tf_op jit(solution)/shard_map/ppermute | solution.py:18
  426.8 4.7 collective-permute-start.1
  435.6 13.4 %collective-permute-start.2 = (f32[12,4,188]{2,1,0:T(4,128)}, f32[12,4,188]{2,1,0:T(4,128)}, u32[]{:S(2)}, u32[]{:S(2)}) collective-permute-start(f32[12,4,188]{2,1,0:T(4,128)} %copy.45), channel_id=1, source_target_pairs={{0,8},{8,16},{16,24},{1,9},{9,17},{17,25},{2,10},{10,18},{18,26},{... | collective-permute-start | bytes 108296 | tf_op jit(solution)/shard_map/ppermute | solution.py:18
  440.8 9.4 %collective-permute-start.3 = (f32[12,4,188]{2,1,0:T(4,128)}, f32[12,4,188]{2,1,0:T(4,128)}, u32[]{:S(2)}, u32[]{:S(2)}) collective-permute-start(f32[12,4,188]{2,1,0:T(4,128)} %copy.46), channel_id=1, source_target_pairs={{8,0},{16,8},{24,16},{9,1},{17,9},{25,17},{10,2},{18,10},{26,18},{... | collective-permute-start | bytes 108296 | tf_op jit(solution)/shard_map/ppermute | solution.py:19
  452.5 1.4 copy-start
  459.7 2.1 copy-start.3
  459.7 2.1 copy-start.4
  459.7 2.1 copy-start.5
  459.7 2.1 copy-start.6
Sparse Core Ops, SparseCore 0:
  10.1 38.2 all-gather.1
  314.1 107.8 all-reduce.1
where the time goes:
time: 474 us; the launch traced here: 473 us
  waiting for transfers between devices  292 us (62%)
  local copies, waits for them, and re-layouts  84.6 us (18%)
  other arithmetic  31.8 us (7%)
  matrix products  23 us (5%)
  starting transfers between devices  16 us (3%)
  between operations  14.3 us (3%)
  blocking collectives  10.5 us (2%)
    all_to_all x1, waiting for transfers between devices, per_device(): lax.all_to_all(along_lon, 'lat', split_axis=3, concat_axis=0, tiled=True)  150 us
    psum x1, waiting for transfers between devices, per_device(): lax.psum(jnp.sum(localized * pert_rows.astype(jnp.float32), axis=1) * ens...  102 us
    all_gather x1, waiting for transfers between devices, per_device(): lax.all_gather(lon_loc, 'mem', axis=1, tiled=True)  38.8 us
    convert_element_type x1, local copies, waits for them, and re-layouts, per_device(): along_lon = jnp.einsum('mfal,lc->amfc', control, lax.all_gather(lon_loc,...  16.8 us
    dot_general x1, matrix products, per_device(): jnp.einsum('mfal,lc->amfc', control, lax.all_gather(lon_loc, 'mem', axis=...  13.5 us
    unnamed x22, local copies, waits for them, and re-layouts  12.6 us
    reshape x1, local copies, waits for them, and re-layouts, per_device(): flat_band = banded.reshape(banded.shape[0], mem_here * fields * lon_width)  12.2 us
    dot_general x1, local copies, waits for them, and re-layouts, per_device(): jnp.dot(lat_weights_all, flat_band, preferred_element_type=jnp.float32)  11.8 us
  transfers between devices with their start and end apart: 7, of which 4 were waited for; matrix products, arithmetic and copies ran while one was open for 3% of the time, Pallas kernels for 0%

commit v1 on v0

--- a/solution.py
+++ b/solution.py
@@ -63,7 +63,9 @@
     along_lon = jnp.einsum(
         "mfal,lc->amfc",
         control,
-        lax.all_gather(lon_loc, "mem", axis=1, tiled=True),
+        jnp.concatenate(
+            lax.all_to_all(jnp.stack([lon_loc] * lax.axis_size("mem")), "mem", 0, 0), axis=1
+        ),
         preferred_element_type=jnp.float32,
     ).astype(jnp.bfloat16)
     banded = lax.all_to_all(along_lon, "lat", split_axis=3, concat_axis=0, tiled=True)

time: 474 us -> 510 us (1.076)
  blocking collectives: 10.5 us -> 64.2 us
  waiting for transfers between devices: 292 us -> 254 us
  local copies, waits for them, and re-layouts: 84.6 us -> 105 us
    all_to_all x0 -> x1, blocking collectives: none -> 53.7 us  [per_device(): lax.all_to_all(jnp.stack([lon_loc] * lax.axis_size('mem')), 'mem', 0, 0)]
    all_gather x1 -> x0, waiting for transfers between devices: 38.8 us -> none  [per_device(): lax.all_gather(lon_loc, 'mem', axis=1, tiled=True)]
    reshape x0 -> x2, local copies, waits for them, and re-layouts: none -> 20.7 us  [per_device(): jnp.concatenate(lax.all_to_all(jnp.stack([lon_loc] * lax.axis_size('mem')...]
    unnamed x22 -> x21, local copies, waits for them, and re-layouts: 12.6 us -> 10.3 us
  transfers between devices with their start and end apart: 7 -> 6, of which waited for: 4 -> 3; matrix products, arithmetic and copies ran while one was open for 3% -> 3% of each run, Pallas kernels for 0% -> 0%
where the time goes in v1:
time: 510 us; the launch traced here: 508 us
  waiting for transfers between devices  254 us (50%)
  local copies, waits for them, and re-layouts  105 us (21%)
  blocking collectives  64.2 us (13%)
  other arithmetic  31.8 us (6%)
  matrix products  22.9 us (4%)
  starting transfers between devices  16.2 us (3%)
  between operations  14.3 us (3%)
    all_to_all x1, waiting for transfers between devices, per_device(): lax.all_to_all(along_lon, 'lat', split_axis=3, concat_axis=0, tiled=True)  150 us
    psum x1, waiting for transfers between devices, per_device(): lax.psum(jnp.sum(localized * pert_rows.astype(jnp.float32), axis=1) * ens...  102 us
    all_to_all x1, blocking collectives, per_device(): lax.all_to_all(jnp.stack([lon_loc] * lax.axis_size('mem')), 'mem', 0, 0)  53.7 us
    reshape x2, local copies, waits for them, and re-layouts, per_device(): jnp.concatenate(lax.all_to_all(jnp.stack([lon_loc] * lax.axis_size('mem')...  20.7 us
    convert_element_type x1, local copies, waits for them, and re-layouts, per_device(): along_lon = jnp.einsum('mfal,lc->amfc', control, jnp.concatenate(lax.all_...  16.8 us
    dot_general x1, matrix products, per_device(): jnp.einsum('mfal,lc->amfc', control, jnp.concatenate(lax.all_to_all(jnp.s...  13.4 us
    reshape x1, local copies, waits for them, and re-layouts, per_device(): flat_band = banded.reshape(banded.shape[0], mem_here * fields * lon_width)  12.2 us
    dot_general x1, local copies, waits for them, and re-layouts, per_device(): jnp.dot(lat_weights_all, flat_band, preferred_element_type=jnp.float32)  11.8 us
  transfers between devices with their start and end apart: 6, of which 3 were waited for; matrix products, arithmetic and copies ran while one was open for 3% of the time, Pallas kernels for 0%

profile of v1, /device:TPU:1, one launch (start us, length us, event | category | flops | bytes accessed | tf_op | source)
XLA Modules:
  0.0 508.0 jit_solution(11755760181248296988)
XLA Ops:
  7.2 1.6 stack.2
  8.8 53.7 %all_to_all.20 = bf16[4,1440,360]{2,1,0:T(8,128)(2,1)S(1)} all-to-all(bf16[4,1440,360]{2,1,0:T(8,128)(2,1)S(1)} %stack.2), channel_id=1, replica_groups=mesh['mem'=4,'lat'=8] {'mem'}, dimensions={0} | all-to-all | bytes 8294400 | tf_op jit(solution)/shard_map/all_to_all | solution.py:67
  62.5 12.0 %copy.31 = bf16[1440,4,360]{2,1,0:T(4,128)(2,1)} copy(bf16[1440,4,360]{2,0,1:T(8,128)(2,1)S(1)} %bitcast.60) | data formatting | bytes 8294400 | tf_op jit(solution)/shard_map/reshape | solution.py:66
  74.5 8.7 %reshape.23 = bf16[1440,1440,1,1]{1,0,2,3:T(8,128)(2,1)} reshape(bf16[1440,4,360]{2,1,0:T(4,128)(2,1)} %copy.31) | data formatting | bytes 8294400 | tf_op jit(solution)/shard_map/reshape | solution.py:66
  83.2 13.4 %convert_bitcast_fusion = bf16[88,2,10,1440]{3,0,2,1:T(8,128)(2,1)} fusion(bf16[2,10,88,1440]{3,2,1,0:T(8,128)(2,1)} %param.7, bf16[1440,1440,1,1]{1,0,2,3:T(8,128)(2,1)} %reshape.23), kind=kOutput, calls=%fused_computation.4 | convolution fusion | flops 7301606400 | bytes 14284800 | tf_op jit(solution)/shard_map/mfal,lc->amfc/dot_general | solution.py:63
  96.6 16.8 %copy.32 = bf16[88,2,10,1440]{0,1,2,3:T(2,128)(2,1)} copy(bf16[88,2,10,1440]{3,0,2,1:T(8,128)(2,1)} %convert_bitcast_fusion) | data formatting | bytes 10137600 | tf_op jit(solution)/shard_map/convert_element_type | solution.py:70
  113.4 5.7 %all-to-all-start.1 = ((bf16[88,2,10,1440]{0,1,2,3:T(2,128)(2,1)}), bf16[88,2,10,1440]{0,1,2,3:T(2,128)(2,1)}, u32[]{:S(2)}, u32[]{:S(2)}) async-start(bf16[88,2,10,1440]{0,1,2,3:T(2,128)(2,1)} %copy.32), calls=%async_computation.1 | async-start | bytes 14745600 | tf_op jit(solution)/shard_map/all_to_all | solution.py:71
  119.1 0.0 all-reduce.2.cloned.1.call-start
  119.2 0.0 copy-done.7
  119.2 10.5 %all_gather.3 = bf16[704,704]{1,0:T(8,128)(2,1)S(1)} all-gather(bf16[176,704]{1,0:T(8,128)(2,1)S(1)} %copy-done.7), channel_id=1, replica_groups=mesh['mem'=4,'lat'=8] {'mem'}, dimensions={0}, use_global_device_ids=true | all-gather | bytes 1239040 | tf_op jit(solution)/shard_map/all_gather | solution.py:77
  129.7 149.8 %all-to-all-done.1 = bf16[88,2,10,1440]{0,1,2,3:T(2,128)(2,1)} async-done(((bf16[88,2,10,1440]{0,1,2,3:T(2,128)(2,1)}), bf16[88,2,10,1440]{0,1,2,3:T(2,128)(2,1)}, u32[]{:S(2)}, u32[]{:S(2)}) %all-to-all-start.1) | async-done | bytes 5068832 | tf_op jit(solution)/shard_map/all_to_all | solution.py:71
  279.5 8.0 %copy.56 = bf16[88,2,10,8,180]{0,3,4,2,1:T(8,128)(2,1)} copy(bf16[88,2,10,8,180]{0,1,2,4,3:T(2,128)(2,1)} %bitcast.3) | data formatting | bytes 10137600 | tf_op jit(solution)/shard_map/all_to_all | solution.py:71
  287.5 12.2 %reshape.21 = bf16[704,3600]{0,1:T(8,128)(2,1)} reshape(bf16[8,88,2,10,180]{1,0,4,3,2:T(8,128)(2,1)} %bitcast.59) | data formatting | bytes 10137600 | tf_op jit(solution)/shard_map/reshape | solution.py:75
  299.7 9.5 %convolution_bitcast_fusion = f32[704,3600]{1,0:T(8,128)} fusion(bf16[704,3600]{0,1:T(8,128)(2,1)} %reshape.21, bf16[704,704]{1,0:T(8,128)(2,1)S(1)} %all_gather.3), kind=kOutput, calls=%fused_computation.3 | convolution fusion | flops 3568435200 | bytes 16197632 | tf_op jit(solution)/shard_map/dot_general | solution.py:81
  309.2 11.8 %copy.34 = f32[704,3600]{0,1:T(8,128)} copy(f32[704,3600]{1,0:T(8,128)} %convolution_bitcast_fusion) | data formatting | bytes 20275200 | tf_op jit(solution)/shard_map/dot_general | solution.py:81
  321.1 11.6 %reshape.22 = f32[704,2,10,180]{0,3,2,1:T(8,128)} reshape(f32[704,3600]{0,1:T(8,128)} %copy.34) | data formatting | bytes 20275200 | tf_op jit(solution)/shard_map/reshape | solution.py:82
  332.7 10.3 %fusion = f32[704,10,180]{0,2,1:T(8,128)} fusion(f32[704,2,10,180]{0,3,2,1:T(8,128)} %reshape.22, bf16[2,10,704,180]{2,0,3,1:T(2,128)(2,1)} %param.8), kind=kLoop, calls=%fused_computation.1 | loop fusion | flops 6336000 | bytes 20275200 | tf_op jit(solution)/shard_map/reduce_sum | solution.py:84
  343.0 5.5 %broadcast_multiply_fusion = f32[704,10,180]{0,2,1:T(8,128)} fusion(f32[704,10,180]{0,2,1:T(8,128)} %fusion), kind=kLoop, calls=%fused_computation.6 | loop fusion | flops 1267200 | bytes 10137600 | tf_op jit(solution)/shard_map/mul | solution.py:84
  348.5 0.0 all-reduce.2.cloned.1.call-update
  348.5 1.5 copy-done.1
  350.0 1.8 copy.36
  351.8 3.0 copy.37
  354.8 0.0 copy-done.2
  354.8 0.2 copy.38
  355.0 102.3 %all-reduce.2.cloned.1.call-done = f32[704,10,180]{0,2,1:T(8,128)} async-done(((f32[704,10,180]{0,2,1:T(8,128)}), f32[704,10,180]{0,2,1:T(8,128)}) %all-reduce.2.cloned.1.call-update) | async-done | bytes 5068816 | tf_op jit(solution)/shard_map/psum | solution.py:84
  457.3 3.5 bitcast_add_fusion
  460.9 1.2 collective-permute-start
  462.1 3.0 collective-permute-start.1
  465.2 1.6 collective-permute-done
  466.8 0.0 collective-permute-done.1
  466.9 0.3 pad_maximum_fusion
  467.1 1.4 fusion.34
  468.6 2.4 copy.43
  470.9 4.1 collective-permute-start.2
  475.1 1.1 copy.44
  476.2 2.1 collective-permute-start.3
  478.3 1.1 maximum_bitcast_fusion.7
  479.4 0.8 copy.47
  480.2 0.8 copy.48
  480.9 0.8 copy.49
  481.7 0.8 copy.50
  482.5 1.8 copy.51
  484.4 0.0 collective-permute-done.2
  484.4 1.2 copy.45
  485.6 0.0 collective-permute-done.3
  485.6 2.2 copy.46
  487.8 1.3 maximum_bitcast_fusion.3
  489.2 0.0 copy-done
  489.2 0.3 maximum_bitcast_fusion.5
  489.5 0.3 maximum_bitcast_fusion.1
  489.8 1.0 pad_maximum_fusion.1
  490.9 2.1 fusion.4
  493.0 2.0 fusion.28
  495.1 0.0 copy-start.3
  495.1 0.0 copy-start.4
  495.1 0.0 copy-start.5
  495.1 0.0 copy-start.6
  495.1 2.1 fusion.20
  497.2 0.0 copy-done.3
  497.2 0.0 copy-done.4
  497.2 0.0 copy-done.5
  497.2 0.0 copy-done.6
  497.2 2.1 fusion.12
  499.3 1.8 copy.52
  (12 shorter events, 0.2 us)
Async XLA Ops:
  113.4 5.7 %copy-start.7 = (bf16[176,704]{1,0:T(8,128)(2,1)S(1)}, bf16[176,704]{1,0:T(8,128)(2,1)}, u32[]{:S(2)}) copy-start(bf16[176,704]{1,0:T(8,128)(2,1)} %param.10) | copy-start | bytes 743428
  113.4 166.0 %all-to-all-start.1 = ((bf16[88,2,10,1440]{0,1,2,3:T(2,128)(2,1)}), bf16[88,2,10,1440]{0,1,2,3:T(2,128)(2,1)}, u32[]{:S(2)}, u32[]{:S(2)}) async-start(bf16[88,2,10,1440]{0,1,2,3:T(2,128)(2,1)} %copy.32), calls=%async_computation.1 | async-start | bytes 14745600 | tf_op jit(solution)/shard_map/all_to_all | solution.py:71
  119.1 338.2 %all-reduce.2.cloned.1.call-start = ((), (), s32[]{:S(2)}) async-start(), calls=%async_computation.2 | async-start | bytes 11304960 | tf_op jit(solution)/shard_map/psum | solution.py:84
  348.5 1.5 copy-start.1
  351.8 3.0 copy-start.2
  460.9 5.9 %collective-permute-start = (f32[12,176,4]{1,0,2:T(8,128)S(1)}, f32[12,176,4]{1,0,2:T(8,128)S(1)}, u32[]{:S(2)}, u32[]{:S(2)}) collective-permute-start(f32[12,176,4]{1,0,2:T(8,128)S(1)} %copy.39), channel_id=1, source_target_pairs={{0,1},{1,2},{2,3},{3,4},{4,5},{5,6},{6,7},{7,0},{8,9},{9,10},{10,1... | collective-permute-start | bytes 101384 | tf_op jit(solution)/shard_map/ppermute | solution.py:18
  462.1 4.7 collective-permute-start.1
  470.9 13.4 %collective-permute-start.2 = (f32[12,4,188]{2,1,0:T(4,128)}, f32[12,4,188]{2,1,0:T(4,128)}, u32[]{:S(2)}, u32[]{:S(2)}) collective-permute-start(f32[12,4,188]{2,1,0:T(4,128)} %copy.43), channel_id=1, source_target_pairs={{0,8},{8,16},{16,24},{1,9},{9,17},{17,25},{2,10},{10,18},{18,26},{... | collective-permute-start | bytes 108296 | tf_op jit(solution)/shard_map/ppermute | solution.py:18
  476.2 9.4 %collective-permute-start.3 = (f32[12,4,188]{2,1,0:T(4,128)}, f32[12,4,188]{2,1,0:T(4,128)}, u32[]{:S(2)}, u32[]{:S(2)}) collective-permute-start(f32[12,4,188]{2,1,0:T(4,128)} %copy.44), channel_id=1, source_target_pairs={{8,0},{16,8},{24,16},{9,1},{17,9},{25,17},{10,2},{18,10},{26,18},{... | collective-permute-start | bytes 108296 | tf_op jit(solution)/shard_map/ppermute | solution.py:19
  487.8 1.4 copy-start
  495.1 2.1 copy-start.3
  495.1 2.1 copy-start.4
  495.1 2.1 copy-start.5
  495.1 2.1 copy-start.6
Sparse Core Ops, SparseCore 0:
  348.6 108.6 all-reduce.1
